TPU v7x, 32 devices: a whole 2x2x4 slice. The times are simulated.
32 devices in a mesh: member: 4 (over z), py: 4 (over x, core), pz: 2 (over y).
Axes of the slice: x: 2, y: 2, z: 4, core: 2. Of those that a mesh axis runs over, the one named last changes fastest.
Arguments:
- velocity_hat: float32 [8, 3, 96, 36864], P('member', None, None, ('py', 'pz')), parts along dimension 0, may hold values from -448 to 448
- time_step: float32 [4], P('member'), parts along dimension 0, may hold values from 0.003 to 0.006
- power: float32 [4], P('member'), parts along dimension 0, may hold values from 20 to 80
- cutoffs: int32 [12], P('member'), parts along dimension 0, may hold values from 48 to 64, as said below
Outputs:
- velocity_next: float32 [8, 3, 96, 36864], P('member', None, None, ('py', 'pz')), parts along dimension 0
- cfl_number: float32 [4], P('member'), parts along dimension 0
- energy: float32 [4], P('member'), parts along dimension 0
There are 4 independent parts, one for each index of `member`. A program takes and returns all parts, laid end to end along the dimension named above; each array names one. Nothing has to cross between parts.
Inputs may be any that keep to these rules, and one draw needn't show every extreme that they name: `cutoffs`: in every draw one of the three equals 64.
All inputs are finite; a program needn't handle non-finite values.
Results may differ from a plain program's by a relative error of at most 0.0002.
Values sent between devices are 32-bit elements; how exact they have to be, the bound alone decides.
A program may use at most 256 MiB of HBM per device.

v0:
```python
import math

import jax
import jax.numpy as jnp
from jax import lax
from jax.sharding import PartitionSpec as P

viscosity = 0.004
keep_share = (0.0, 0.75, 1.0 / 3.0)
highest = lax.Precision.HIGHEST


def phases(length, row_count, col_count, handed):
    row_index = lax.broadcasted_iota(jnp.int32, (row_count, col_count), 0)
    col_index = lax.broadcasted_iota(jnp.int32, (row_count, col_count), 1)
    windings = row_index * col_index % length
    angles = windings.astype(jnp.float32) * (2.0 * math.pi / length)
    return (jnp.cos(angles), handed * jnp.sin(angles))


def complex_table(length, handed):
    cosine, sine_part = phases(length, length, length, handed)
    return jnp.stack([jnp.stack([cosine, sine_part]), jnp.stack([-sine_part, cosine])])


def depth_tables(length):
    factor = float(length) ** (-1.5)
    cosine, sine_part = phases(length, length // 2, length, 1.0)
    weight = jnp.where(lax.broadcasted_iota(jnp.int32, (length // 2, 1), 0) == 0, 1.0, 2.0)
    backward = jnp.stack([weight * cosine, -weight * sine_part]) * factor
    onward = jnp.stack([cosine.T, -sine_part.T], axis=1) * factor
    return (backward, onward)


def slab_spread(fields, group_size, slab_width, table):
    points = table.shape[-1]
    components, depth_part, cross_part = (fields.shape[1], fields.shape[2], fields.shape[3])
    spread = jnp.einsum(
        "rcjlk,rskgx->scgjlx",
        fields,
        table.reshape(2, 2, points, group_size, slab_width),
        precision=highest,
    )
    return spread.reshape(2, components, group_size, depth_part * cross_part * slab_width)


def slab_finish(received, group_size, depth_part, cross_part, slab_width, table, backward_cut):
    points = table.shape[-1]
    components = received.shape[1]
    pieces = received.reshape(2, components, group_size, depth_part, cross_part, slab_width)
    strips = jnp.einsum(
        "rcgjlx,rsgly->scjxy",
        pieces,
        table.reshape(2, 2, group_size, cross_part, points),
        precision=highest,
    )
    return jnp.einsum("scjxy,sjz->cxyz", strips, backward_cut, precision=highest)


def slab_planes(physical, group_size, cross_part, onward_cut, table):
    components, slab_width, points = (physical.shape[0], physical.shape[1], physical.shape[3])
    depth_part = onward_cut.shape[2]
    planes = jnp.einsum("cxyz,zrj->rcjxy", physical, onward_cut, precision=highest)
    strips = jnp.einsum(
        "rcjxy,rsygl->scgjlx",
        planes,
        table.reshape(2, 2, points, group_size, cross_part),
        precision=highest,
    )
    return strips.reshape(2, components, group_size, depth_part * cross_part * slab_width)


def slab_close(received, group_size, depth_part, cross_part, slab_width, table):
    points = table.shape[-1]
    components = received.shape[1]
    pieces = received.reshape(2, components, group_size, depth_part, cross_part, slab_width)
    return jnp.einsum(
        "scgjlx,srgxk->rcjlk",
        pieces,
        table.reshape(2, 2, group_size, slab_width, points),
        precision=highest,
    )


def on_device(velocity_hat, time_step, power, cutoffs):
    count_y = lax.axis_size("py")
    count_z = lax.axis_size("pz")
    group_size = count_y * count_z
    half_depth = velocity_hat.shape[2]
    points = 2 * half_depth
    cross_part = velocity_hat.shape[3] // points
    flat_width = velocity_hat.shape[3]
    slab_width = points // group_size
    depth_keep = points // 3 + 1
    inverse_table = complex_table(points, 1.0)
    forward_table = complex_table(points, -1.0)
    backward, onward = depth_tables(points)
    backward_cut = backward[:, :depth_keep]
    onward_cut = onward[:, :, :depth_keep]
    depth_wave = lax.broadcasted_iota(jnp.int32, (half_depth, 1, 1), 0)
    cross_index = lax.axis_index(("py", "pz")) * cross_part + lax.broadcasted_iota(
        jnp.int32, (1, cross_part, 1), 1
    )
    cross_wave = jnp.where(cross_index < points // 2, cross_index, cross_index - points)
    along_index = lax.broadcasted_iota(jnp.int32, (1, 1, points), 2)
    along_wave = jnp.where(along_index < points // 2, along_index, along_index - points)
    keep_mask = (
        (jnp.abs(along_wave) <= cutoffs[0])
        & (jnp.abs(cross_wave) <= cutoffs[1])
        & (depth_wave <= cutoffs[2])
    ).astype(jnp.float32)
    waves = (
        along_wave.astype(jnp.float32),
        cross_wave.astype(jnp.float32),
        depth_wave.astype(jnp.float32),
    )
    wave_square = waves[0] * waves[0] + waves[1] * waves[1] + waves[2] * waves[2]
    inverse_square = 1.0 / jnp.maximum(wave_square, 1.0)

    def project(field):
        normal_part = waves[0] * field[:, 0] + waves[1] * field[:, 1] + waves[2] * field[:, 2]
        return jnp.stack(
            [
                keep_mask
                * (field[:, axis_index] - waves[axis_index] * normal_part * inverse_square)
                for axis_index in range(3)
            ],
            axis=1,
        )

    step_size = time_step[0]
    current = velocity_hat.reshape(2, 3, half_depth, cross_part, points)
    solenoidal = project(current)
    curled = jnp.stack(
        [
            waves[1] * solenoidal[:, 2] - waves[2] * solenoidal[:, 1],
            waves[2] * solenoidal[:, 0] - waves[0] * solenoidal[:, 2],
            waves[0] * solenoidal[:, 1] - waves[1] * solenoidal[:, 0],
        ],
        axis=1,
    )
    vorticity_hat = jnp.stack([-curled[1], curled[0]])
    fields = jnp.concatenate([solenoidal, vorticity_hat], axis=1)[:, :, :depth_keep]
    spread = slab_spread(fields, group_size, slab_width, inverse_table)
    physical = slab_finish(
        lax.all_to_all(spread, ("py", "pz"), split_axis=2, concat_axis=2, tiled=True),
        group_size,
        depth_keep,
        cross_part,
        slab_width,
        inverse_table,
        backward_cut,
    )
    velocity = physical[:3]
    vorticity = physical[3:]
    nonlinear = jnp.stack(
        [
            velocity[1] * vorticity[2] - velocity[2] * vorticity[1],
            velocity[2] * vorticity[0] - velocity[0] * vorticity[2],
            velocity[0] * vorticity[1] - velocity[1] * vorticity[0],
        ]
    )
    local_fastest = jnp.max(jnp.abs(velocity[0]) + jnp.abs(velocity[1]) + jnp.abs(velocity[2]))
    local_squares = jnp.sum(velocity * velocity)
    fastest = lax.pmax(local_fastest, ("py", "pz"))
    summed = lax.psum(local_squares, ("py", "pz"))
    energy = 0.5 * summed / float(points**3)
    layers = slab_planes(nonlinear, group_size, cross_part, onward_cut, forward_table)
    spectra = slab_close(
        lax.all_to_all(layers, ("py", "pz"), split_axis=2, concat_axis=2, tiled=True),
        group_size,
        depth_keep,
        cross_part,
        slab_width,
        forward_table,
    )
    spectra = jnp.concatenate(
        [spectra, jnp.zeros((2, 3, half_depth - depth_keep, cross_part, points), jnp.float32)],
        axis=2,
    )
    forced = project(spectra)
    forcing = power[0] / jnp.maximum(2.0 * energy, 0.5)
    update = solenoidal + step_size * (
        forced + forcing * solenoidal - viscosity * wave_square * solenoidal
    )
    keep_weight = keep_share[0]
    current = keep_weight * solenoidal + (1.0 - keep_weight) * update
    cfl_values = [step_size * fastest * points / (2.0 * math.pi)]
    energy_values = [energy]
    velocity_next = current.reshape(2, 3, half_depth, flat_width)
    return (velocity_next, jnp.stack(cfl_values), jnp.stack(energy_values))


def solution(mesh):
    return jax.shard_map(
        on_device,
        mesh=mesh,
        in_specs=(P("member", None, None, ("py", "pz")), P("member"), P("member"), P("member")),
        out_specs=(P("member", None, None, ("py", "pz")), P("member"), P("member")),
        check_vma=False,
    )
```

profile of v0, /device:TPU:0, one launch (start us, length us, event | category | flops | bytes accessed | tf_op | source)
XLA Modules:
  0.0 1035.7 jit_solution(9953990151578628140)
XLA Ops:
  0.8 13.5 %reshape.482 = f32[2,3,96,24,192]{4,3,2,1,0:T(8,128)} reshape(f32[2,3,96,4608]{3,2,1,0:T(8,128)} %param.4) | data formatting | bytes 21233664 | tf_op jit(solution)/shard_map/reshape | solution.py:132
  14.3 10.6 %fusion.108 = (f32[2,1,96,24,192]{4,3,2,1,0:T(8,128)}, f32[2,1,96,24,192]{4,3,2,1,0:T(8,128)}, f32[2,1,96,24,192]{4,3,2,1,0:T(8,128)}) fusion(f32[2,3,96,24,192]{4,3,2,1,0:T(8,128)} %reshape.482), kind=kLoop, calls=%fused_computation.158 | loop fusion | bytes 21233664 | tf_op jit(solution)/shard_map/slice | solution.py:121
  28.8 12.8 %multiply_subtract_fusion.5 = (f32[2,1,96,24,192]{4,2,0,3,1:T(8,128)}, f32[2,1,96,24,192]{4,2,0,3,1:T(8,128)}, f32[2,1,96,24,192]{4,2,0,3,1:T(8,128)}) fusion(f32[96]{0:T(128)S(1)} %iota_convert_fusion, f32[24]{0:T(128)S(1)} %fusion.96, f32[96,24,192]{2,0,1:T(8,128)S(1)} %maximum_divide_fusion, f32[2,1,96,24,192]{4,3,2,1,0:T(8,128)} %get-tuple-element.28, ...), kind=kLoop, calls=%fused_computation.45 | loop fusion | flops 14155776 | bytes 24773856 | tf_op jit(solution)/shard_map/sub | solution.py:136
  41.6 22.7 %multiply_subtract_fusion.4 = (f32[2,1,96,24,192]{4,2,0,3,1:T(8,128)}, f32[2,1,96,24,192]{4,2,0,3,1:T(8,128)}) fusion(f32[2,1,96,24,192]{4,2,0,3,1:T(8,128)} %get-tuple-element.15, f32[96]{0:T(128)S(1)} %iota_convert_fusion, f32[192]{0:T(256)S(1)} %fusion.94, f32[96,24,192]{2,0,1:T(8,128)S(1)} %maximum_divide_fusion, ...), kind=kLoop, calls=%fused_computation.44 | loop fusion | flops 10616832 | bytes 24773856 | tf_op jit(solution)/shard_map/sub | solution.py:137
  71.7 12.6 %pad_maximum_fusion.5 = f32[2,3,96,24,192]{4,2,0,3,1:T(8,128)} fusion(f32[2,1,96,24,192]{4,2,0,3,1:T(8,128)} %multiply_subtract_fusion.3, f32[2,1,96,24,192]{4,2,0,3,1:T(8,128)} %get-tuple-element.17, f32[2,1,96,24,192]{4,2,0,3,1:T(8,128)} %get-tuple-element.14), kind=kLoop, calls=%fused_computation.18 | loop fusion | flops 5308416 | bytes 21233664 | tf_op jit(solution)/shard_map/stack | solution.py:134
  84.3 12.9 %slice_negate_fusion = (f32[1,3,96,24,192]{4,2,0,3,1:T(8,128)}, f32[1,3,96,24,192]{4,2,0,3,1:T(8,128)}) fusion(f32[2,3,96,24,192]{4,2,0,3,1:T(8,128)} %pad_maximum_fusion.5), kind=kLoop, calls=%fused_computation.33 | loop fusion | flops 1327104 | bytes 21233664 | tf_op jit(solution)/shard_map/neg | solution.py:142
  99.5 49.9 %fusion.10 = f32[2,6,8,65,24,24]{3,5,4,1,2,0:T(8,128)} fusion(f32[1,3,96,24,192]{4,2,0,3,1:T(8,128)} %get-tuple-element.26, f32[1,3,96,24,192]{4,2,0,3,1:T(8,128)} %get-tuple-element.25, f32[2,1,96,24,192]{4,2,0,3,1:T(8,128)} %get-tuple-element.15, f32[2,1,96,24,192]{4,2,0,3,1:T(8,128)} %get-tuple-element.16, f32[2,1,96,24,192]{4,2,0,3,1:T(8,128)} %get-tuple-element.18, ...), kind=kOutput, calls=%fused_computation.12 | convolution fusion | flops 16576634880 | bytes 36200448 | tf_op jit(solution)/shard_map/rcjlk,rskgx->scgjlx/dot_general | solution.py:38
  149.4 48.7 %copy.74 = f32[2,6,8,65,24,24]{5,4,3,0,1,2:T(8,128)} copy(f32[2,6,8,65,24,24]{3,5,4,1,2,0:T(8,128)} %fusion.10) | data formatting | bytes 28753920 | tf_op jit(solution)/shard_map/reshape | solution.py:44
  198.1 65.1 %reshape.503 = f32[2,6,8,37440]{3,0,1,2:T(2,128)} reshape(f32[2,6,8,65,24,24]{5,4,3,0,1,2:T(8,128)} %copy.74) | data formatting | bytes 28753920 | tf_op jit(solution)/shard_map/reshape | solution.py:44
  271.7 155.7 %all-to-all-done = f32[2,6,8,37440]{3,0,1,2:T(2,128)} async-done(((f32[2,6,8,37440]{3,0,1,2:T(2,128)}), f32[2,6,8,37440]{3,0,1,2:T(2,128)}, u32[]{:S(2)}, u32[]{:S(2)}) %all-to-all-start) | async-done | bytes 14376992 | tf_op jit(solution)/shard_map/all_to_all | solution.py:146
  427.4 56.7 %reshape.504 = f32[2,6,8,65,24,24]{5,4,3,0,1,2:T(8,128)} reshape(f32[2,6,8,37440]{3,0,1,2:T(2,128)} %all-to-all-done) | data formatting | bytes 28753920 | tf_op jit(solution)/shard_map/reshape | solution.py:50
  484.1 55.9 %copy.62 = f32[2,6,8,65,24,24,1]{3,4,0,2,6,5,1:T(8,128)} copy(f32[2,6,8,65,24,24,1]{5,4,3,0,1,2,6:T(8,128)} %bitcast.19) | data formatting | bytes 28753920 | tf_op jit(solution)/shard_map/reshape | solution.py:50
  540.0 49.3 %fusion.45 = f32[2,192,6,65,24,1,1]{1,3,6,5,0,4,2:T(8,128)S(1)} fusion(f32[2,6,8,65,24,24,1]{3,4,0,2,6,5,1:T(8,128)} %copy.62, f32[1,1,8,24,192]{4,3,0,2,1:T(8,128)S(1)} %get-tuple-element.34, f32[1,1,8,24,192]{4,3,0,2,1:T(8,128)S(1)} %get-tuple-element.32, f32[1,1,8,24,192]{4,3,0,2,1:T(8,128)S(1)} %get-tuple-element.33), kind=kOutput, calls=%fused_computation.70 | convolution fusion | flops 16562700288 | bytes 29196288 | tf_op jit(solution)/shard_map/rcgjlx,rsgly->scjxy/dot_general | solution.py:51
  589.2 55.6 %fusion.25 = f32[6,24,192,192]{3,2,1,0:T(8,128)} fusion(f32[2,192,6,65,24,1,1]{1,3,6,5,0,4,2:T(8,128)S(1)} %fusion.45, f32[1,96,192]{2,1,0:T(8,128)S(1)} %get-tuple-element.43, f32[1,96,192]{2,1,0:T(8,128)S(1)} %get-tuple-element.44), kind=kOutput, calls=%fused_computation.32 | convolution fusion | flops 8281179136 | bytes 35758080 | tf_op jit(solution)/shard_map/scjxy,sjz->cxyz/dot_general | solution.py:57
  644.8 11.2 %add_reduce_fusion = (f32[]{:T(128)}, f32[1,24,192,192]{3,2,1,0:T(8,128)S(1)}, f32[1,24,192,192]{3,2,1,0:T(8,128)S(1)}, f32[1,24,192,192]{3,2,1,0:T(8,128)S(1)}) fusion(f32[6,24,192,192]{3,2,1,0:T(8,128)} %fusion.25), kind=kLoop, calls=%fused_computation.35 | loop fusion | flops 13271039 | bytes 31850500 | tf_op jit(solution)/shard_map/reduce_max | solution.py:163
  656.0 17.5 %fusion.14 = f32[2,65,3,24,192]{4,1,0,3,2:T(8,128)} fusion(f32[1,24,192,192]{3,2,1,0:T(8,128)S(1)} %get-tuple-element.22, f32[1,24,192,192]{3,2,1,0:T(8,128)S(1)} %get-tuple-element.20, f32[1,24,192,192]{3,2,1,0:T(8,128)S(1)} %get-tuple-element.21, f32[192,1,96]{0,2,1:T(8,128)S(1)} %get-tuple-element.45, f32[192,1,96]{0,2,1:T(8,128)S(1)} %get-tuple-element.46), kind=kOutput, calls=%fused_computation.20 | convolution fusion | flops 4145922816 | bytes 17952768 | tf_op jit(solution)/shard_map/cxyz,zrj->rcjxy/dot_general | solution.py:63
  673.5 27.0 %fusion.28 = f32[2,3,8,65,24,24]{3,4,5,1,2,0:T(8,128)} fusion(f32[2,65,3,24,192]{4,1,0,3,2:T(8,128)} %fusion.14, f32[1,1,192,8,24]{2,4,0,3,1:T(8,128)S(1)} %copy-done.9, f32[1,1,192,8,24]{2,4,0,3,1:T(8,128)S(1)} %copy-done.15, f32[1,1,192,8,24]{2,4,0,3,1:T(8,128)S(1)} %copy-done.14), kind=kOutput, calls=%fused_computation.34 | convolution fusion | flops 8281571328 | bytes 14819328 | tf_op jit(solution)/shard_map/rcjxy,rsygl->scgjlx/dot_general | solution.py:64
  700.5 25.9 %copy.79 = f32[2,3,8,65,24,24]{5,4,3,0,1,2:T(8,128)} copy(f32[2,3,8,65,24,24]{3,4,5,1,2,0:T(8,128)} %fusion.28) | data formatting | bytes 14376960 | tf_op jit(solution)/shard_map/reshape | solution.py:70
  726.4 33.4 %reshape.505 = f32[2,3,8,37440]{3,0,1,2:T(2,128)} reshape(f32[2,3,8,65,24,24]{5,4,3,0,1,2:T(8,128)} %copy.79) | data formatting | bytes 14376960 | tf_op jit(solution)/shard_map/reshape | solution.py:70
  810.9 9.3 fusion.13
  820.8 32.4 %psum.7 = f32[]{:T(128)} all-reduce(f32[]{:T(128)} %fusion.13), channel_id=1, replica_groups=mesh['member'=4,'py'=4,'pz'=2] {'py','pz'}, use_global_device_ids=true, to_apply=%region_1.2 | all-reduce | flops 1 | bytes 8 | tf_op jit(solution)/shard_map/psum | solution.py:166
  853.3 14.3 %pmax.7 = f32[]{:T(128)} all-reduce(f32[]{:T(128)} %get-tuple-element.19), channel_id=1, replica_groups=mesh['member'=4,'py'=4,'pz'=2] {'py','pz'}, use_global_device_ids=true, to_apply=%region_3.4 | all-reduce | flops 1 | bytes 8 | tf_op jit(solution)/shard_map/pmax | solution.py:165
  869.4 29.4 %reshape.506 = f32[2,3,8,65,24,24]{5,4,3,0,1,2:T(8,128)} reshape(f32[2,3,8,37440]{3,0,1,2:T(2,128)} %all-to-all-done.1) | data formatting | bytes 14376960 | tf_op jit(solution)/shard_map/reshape | solution.py:76
  898.9 80.2 %fusion.31 = f32[2,3,65,24,192]{4,2,0,3,1:T(8,128)S(1)} fusion(f32[2,3,8,65,24,24,1]{5,4,3,0,1,2,6:T(8,128)} %bitcast.149, f32[1,1,8,24,192]{4,3,0,2,1:T(8,128)S(1)} %copy-done.7, f32[1,1,8,24,192]{4,3,0,2,1:T(8,128)S(1)} %copy-done.13, f32[1,1,8,24,192]{4,3,0,2,1:T(8,128)S(1)} %copy-done.12), kind=kOutput, calls=%fused_computation.50 | convolution fusion | flops 8281571328 | bytes 14819328 | tf_op jit(solution)/shard_map/scgjlx,srgxk->rcjlk/dot_general | solution.py:77
  (114 shorter events, 126.6 us)
Async XLA Ops:
  0.6 40.9 %copy-start.21 = (f32[96]{0:T(128)}, f32[96]{0:T(128)S(1)}, u32[]{:S(2)}) copy-start(f32[96]{0:T(128)S(1)} %iota_convert_fusion) | copy-start | bytes 1156
  0.7 27.0 %copy-start.24 = (f32[96]{0:T(128)}, f32[96]{0:T(128)S(1)}, u32[]{:S(2)}) copy-start(f32[96]{0:T(128)S(1)} %fusion.97) | copy-start | bytes 1156
  0.7 63.6 %copy-start.19 = (f32[24]{0:T(128)}, f32[24]{0:T(128)S(1)}, u32[]{:S(2)}) copy-start(f32[24]{0:T(128)S(1)} %fusion.96) | copy-start | bytes 292
  0.7 63.6 %copy-start.17 = (f32[192]{0:T(256)}, f32[192]{0:T(256)S(1)}, u32[]{:S(2)}) copy-start(f32[192]{0:T(256)S(1)} %fusion.94) | copy-start | bytes 2308
  28.3 13.2 %copy-start = (f32[96,24,192]{2,0,1:T(8,128)}, f32[96,24,192]{2,0,1:T(8,128)S(1)}, u32[]{:S(2)}) copy-start(f32[96,24,192]{2,0,1:T(8,128)S(1)} %maximum_divide_fusion) | copy-start | bytes 5308420
  28.4 13.2 %slice-start = ((s8[4718592]{0:T(1024)(128)(4,1)}), s8[4194304]{0:T(1024)(128)(4,1)S(1)}, s32[]{:S(2)}) async-start(s8[4718592]{0:T(1024)(128)(4,1)} %bitcast.143), calls=%async_computation.2 | async-start | bytes 8388608
  28.4 13.2 %slice-start.2 = ((s8[4718592]{0:T(1024)(128)(4,1)}), s8[4194304]{0:T(1024)(128)(4,1)S(1)}, s32[]{:S(2)}) async-start(s8[4718592]{0:T(1024)(128)(4,1)} %bitcast.145), calls=%async_computation.4 | async-start | bytes 8388608
  28.8 12.8 %slice-start.1 = ((s8[4718592]{0:T(1024)(128)(4,1)}), s8[524288]{0:T(1024)(128)(4,1)S(1)}, s32[]{:S(2)}) async-start(s8[4718592]{0:T(1024)(128)(4,1)} %bitcast.143), calls=%async_computation.3 | async-start | bytes 1048576
  28.8 12.8 %slice-start.3 = ((s8[4718592]{0:T(1024)(128)(4,1)}), s8[524288]{0:T(1024)(128)(4,1)S(1)}, s32[]{:S(2)}) async-start(s8[4718592]{0:T(1024)(128)(4,1)} %bitcast.145), calls=%async_computation.5 | async-start | bytes 1048576
  263.2 164.2 %all-to-all-start = ((f32[2,6,8,37440]{3,0,1,2:T(2,128)}), f32[2,6,8,37440]{3,0,1,2:T(2,128)}, u32[]{:S(2)}, u32[]{:S(2)}) async-start(f32[2,6,8,37440]{3,0,1,2:T(2,128)} %reshape.503), calls=%async_computation | async-start | bytes 28803072 | tf_op jit(solution)/shard_map/all_to_all | solution.py:146
  271.6 268.3 %copy-start.6 = (f32[1,1,8,24,192]{4,3,0,2,1:T(8,128)}, f32[1,1,8,24,192]{4,3,0,2,1:T(8,128)S(1)}, u32[]{:S(2)}) copy-start(f32[1,1,8,24,192]{4,3,0,2,1:T(8,128)S(1)} %get-tuple-element.34) | copy-start | bytes 442372
  656.0 17.5 %copy-start.9 = (f32[1,1,192,8,24]{2,4,0,3,1:T(8,128)S(1)}, f32[1,1,192,8,24]{2,4,0,3,1:T(8,128)}, u32[]{:S(2)}) copy-start(f32[1,1,192,8,24]{2,4,0,3,1:T(8,128)} %copy-done.8) | copy-start | bytes 442372
  656.0 17.5 %copy-start.14 = (f32[1,1,192,8,24]{2,4,0,3,1:T(8,128)S(1)}, f32[1,1,192,8,24]{2,4,0,3,1:T(8,128)}, u32[]{:S(2)}) copy-start(f32[1,1,192,8,24]{2,4,0,3,1:T(8,128)} %get-tuple-element.35) | copy-start | bytes 442372
  656.0 17.5 %copy-start.15 = (f32[1,1,192,8,24]{2,4,0,3,1:T(8,128)S(1)}, f32[1,1,192,8,24]{2,4,0,3,1:T(8,128)}, u32[]{:S(2)}) copy-start(f32[1,1,192,8,24]{2,4,0,3,1:T(8,128)} %get-tuple-element.36) | copy-start | bytes 442372
  759.8 109.5 %all-to-all-start.1 = ((f32[2,3,8,37440]{3,0,1,2:T(2,128)}), f32[2,3,8,37440]{3,0,1,2:T(2,128)}, u32[]{:S(2)}, u32[]{:S(2)}) async-start(f32[2,3,8,37440]{3,0,1,2:T(2,128)} %reshape.505), calls=%async_computation.1 | async-start | bytes 14401536 | tf_op jit(solution)/shard_map/all_to_all | solution.py:170
  764.8 14.7 %slice-start.4 = ((s8[4718592]{0:T(1024)(128)(4,1)}), s8[4194304]{0:T(1024)(128)(4,1)S(1)}, s32[]{:S(2)}) async-start(s8[4718592]{0:T(1024)(128)(4,1)} %bitcast.147), calls=%async_computation.6 | async-start | bytes 8388608
  869.3 29.5 %copy-start.7 = (f32[1,1,8,24,192]{4,3,0,2,1:T(8,128)S(1)}, f32[1,1,8,24,192]{4,3,0,2,1:T(8,128)}, u32[]{:S(2)}) copy-start(f32[1,1,8,24,192]{4,3,0,2,1:T(8,128)} %copy-done.6) | copy-start | bytes 442372
  869.3 29.5 %copy-start.12 = (f32[1,1,8,24,192]{4,3,0,2,1:T(8,128)S(1)}, f32[1,1,8,24,192]{4,3,0,2,1:T(8,128)}, u32[]{:S(2)}) copy-start(f32[1,1,8,24,192]{4,3,0,2,1:T(8,128)} %get-tuple-element.30) | copy-start | bytes 442372
  869.3 29.5 %copy-start.13 = (f32[1,1,8,24,192]{4,3,0,2,1:T(8,128)S(1)}, f32[1,1,8,24,192]{4,3,0,2,1:T(8,128)}, u32[]{:S(2)}) copy-start(f32[1,1,8,24,192]{4,3,0,2,1:T(8,128)} %get-tuple-element.31) | copy-start | bytes 442372
  898.8 80.2 %copy-start.1 = (f32[96,24,192]{2,0,1:T(8,128)S(1)}, f32[96,24,192]{2,0,1:T(8,128)}, u32[]{:S(2)}) copy-start(f32[96,24,192]{2,0,1:T(8,128)} %copy-done) | copy-start | bytes 5308420
  898.8 80.2 %copy-start.3 = (f32[96,24,192]{2,0,1:T(8,128)S(1)}, f32[96,24,192]{2,0,1:T(8,128)}, u32[]{:S(2)}) copy-start(f32[96,24,192]{2,0,1:T(8,128)} %copy-done.2) | copy-start | bytes 5308420
  898.8 80.2 %copy-start.18 = (f32[192]{0:T(256)S(1)}, f32[192]{0:T(256)}, u32[]{:S(2)}) copy-start(f32[192]{0:T(256)} %copy-done.17) | copy-start | bytes 2308
  898.8 80.2 %copy-start.20 = (f32[24]{0:T(128)S(1)}, f32[24]{0:T(128)}, u32[]{:S(2)}) copy-start(f32[24]{0:T(128)} %copy-done.19) | copy-start | bytes 292
  898.8 80.2 %copy-start.22 = (f32[96]{0:T(128)S(1)}, f32[96]{0:T(128)}, u32[]{:S(2)}) copy-start(f32[96]{0:T(128)} %copy-done.21) | copy-start | bytes 1156
  (10 other events, 49.8 us)
where the time goes:
time: 1050 us; the launch traced here: 1040 us
  local copies, waits for them, and re-layouts  424 us (40%)
  matrix products  279 us (27%)
  waiting for transfers between devices  156 us (15%)
  other arithmetic  112 us (11%)
  blocking collectives  46.7 us (4%)
  starting transfers between devices  10.9 us (1%)
    all_to_all x1, waiting for transfers between devices, on_device(): lax.all_to_all(spread, ('py', 'pz'), split_axis=2, concat_axis=2, tiled=T...  156 us
    reshape x2, local copies, waits for them, and re-layouts, slab_spread(): spread.reshape(2, components, group_size, depth_part * cross_part * slab_...  114 us
    reshape x2, local copies, waits for them, and re-layouts, slab_finish(): received.reshape(2, components, group_size, depth_part, cross_part, slab_...  113 us
    dot_general x1, matrix products, slab_close(): jnp.einsum('scgjlx,srgxk->rcjlk', pieces, table.reshape(2, 2, group_size,...  80.2 us
    reshape x2, local copies, waits for them, and re-layouts, slab_planes(): strips.reshape(2, components, group_size, depth_part * cross_part * slab_...  59.3 us
    dot_general x1, matrix products, slab_finish(): jnp.einsum('scjxy,sjz->cxyz', strips, backward_cut, precision=highest)  55.6 us
    dot_general x1, matrix products, slab_spread(): jnp.einsum('rcjlk,rskgx->scgjlx', fields, table.reshape(2, 2, points, gro...  49.9 us
    dot_general x1, matrix products, slab_finish(): jnp.einsum('rcgjlx,rsgly->scjxy', pieces, table.reshape(2, 2, group_size,...  49.3 us
  transfers between devices with their start and end apart: 2, of which 1 were waited for; matrix products, arithmetic and copies ran while one was open for 6% of the time, Pallas kernels for 0%

commit v1 on v0

--- a/solution.py
+++ b/solution.py
@@ -7,7 +7,7 @@
 
 viscosity = 0.004
 keep_share = (0.0, 0.75, 1.0 / 3.0)
-highest = lax.Precision.HIGHEST
+highest = lax.Precision.HIGH
 
 
 def phases(length, row_count, col_count, handed):
@@ -34,52 +34,49 @@
 
 def slab_spread(fields, group_size, slab_width, table):
     points = table.shape[-1]
-    components, depth_part, cross_part = (fields.shape[1], fields.shape[2], fields.shape[3])
-    spread = jnp.einsum(
-        "rcjlk,rskgx->scgjlx",
+    return jnp.einsum(
+        "rmlk,rskgx->gsxlm",
         fields,
         table.reshape(2, 2, points, group_size, slab_width),
         precision=highest,
     )
-    return spread.reshape(2, components, group_size, depth_part * cross_part * slab_width)
-
-
-def slab_finish(received, group_size, depth_part, cross_part, slab_width, table, backward_cut):
+
+
+def slab_rows(received, group_size, cross_part, table, components):
     points = table.shape[-1]
-    components = received.shape[1]
-    pieces = received.reshape(2, components, group_size, depth_part, cross_part, slab_width)
     strips = jnp.einsum(
-        "rcgjlx,rsgly->scjxy",
-        pieces,
+        "grxlm,rsgly->sxmy",
+        received,
         table.reshape(2, 2, group_size, cross_part, points),
         precision=highest,
     )
-    return jnp.einsum("scjxy,sjz->cxyz", strips, backward_cut, precision=highest)
+    return strips.reshape(2, strips.shape[1], components, -1, points)
 
 
 def slab_planes(physical, group_size, cross_part, onward_cut, table):
     components, slab_width, points = (physical.shape[0], physical.shape[1], physical.shape[3])
     depth_part = onward_cut.shape[2]
-    planes = jnp.einsum("cxyz,zrj->rcjxy", physical, onward_cut, precision=highest)
-    strips = jnp.einsum(
-        "rcjxy,rsygl->scgjlx",
-        planes,
+    planes = jnp.einsum("cxyz,zrj->rxcjy", physical, onward_cut, precision=highest)
+    return jnp.einsum(
+        "rxmy,rsygl->gsxlm",
+        planes.reshape(2, slab_width, components * depth_part, points),
         table.reshape(2, 2, points, group_size, cross_part),
         precision=highest,
     )
-    return strips.reshape(2, components, group_size, depth_part * cross_part * slab_width)
-
-
-def slab_close(received, group_size, depth_part, cross_part, slab_width, table):
+
+
+def slab_close(received, group_size, slab_width, table):
     points = table.shape[-1]
-    components = received.shape[1]
-    pieces = received.reshape(2, components, group_size, depth_part, cross_part, slab_width)
     return jnp.einsum(
-        "scgjlx,srgxk->rcjlk",
-        pieces,
+        "gsxlm,srgxk->rmlk",
+        received,
         table.reshape(2, 2, group_size, slab_width, points),
         precision=highest,
     )
+
+
+def turned(field):
+    return jnp.stack([-field[1], field[0]])
 
 
 def on_device(velocity_hat, time_step, power, cutoffs):
@@ -91,7 +88,7 @@
     cross_part = velocity_hat.shape[3] // points
     flat_width = velocity_hat.shape[3]
     slab_width = points // group_size
-    depth_keep = points // 3 + 1
+    depth_keep = min(half_depth, (points // 3 + 8) // 8 * 8)
     inverse_table = complex_table(points, 1.0)
     forward_table = complex_table(points, -1.0)
     backward, onward = depth_tables(points)
@@ -131,26 +128,45 @@
     step_size = time_step[0]
     current = velocity_hat.reshape(2, 3, half_depth, cross_part, points)
     solenoidal = project(current)
-    curled = jnp.stack(
+    kept = solenoidal[:, :, :depth_keep]
+    fields = jnp.concatenate(
         [
-            waves[1] * solenoidal[:, 2] - waves[2] * solenoidal[:, 1],
-            waves[2] * solenoidal[:, 0] - waves[0] * solenoidal[:, 2],
-            waves[0] * solenoidal[:, 1] - waves[1] * solenoidal[:, 0],
+            kept,
+            turned(waves[0] * kept[:, 2])[:, None],
+            turned(waves[0] * kept[:, 1] - waves[1] * kept[:, 0])[:, None],
         ],
         axis=1,
-    )
-    vorticity_hat = jnp.stack([-curled[1], curled[0]])
-    fields = jnp.concatenate([solenoidal, vorticity_hat], axis=1)[:, :, :depth_keep]
-    spread = slab_spread(fields, group_size, slab_width, inverse_table)
-    physical = slab_finish(
-        lax.all_to_all(spread, ("py", "pz"), split_axis=2, concat_axis=2, tiled=True),
-        group_size,
-        depth_keep,
-        cross_part,
-        slab_width,
-        inverse_table,
-        backward_cut,
-    )
+    ).reshape(2, 5 * depth_keep, cross_part, points)
+    received = lax.all_to_all(
+        slab_spread(fields, group_size, slab_width, inverse_table),
+        ("py", "pz"),
+        split_axis=0,
+        concat_axis=0,
+        tiled=True,
+    )
+    row_index = lax.broadcasted_iota(jnp.int32, (points, 1), 0)
+    row_wave = jnp.where(row_index < points // 2, row_index, row_index - points)
+    row_wave = row_wave.astype(jnp.float32)
+    slope_table = jnp.stack(
+        [-row_wave * inverse_table[:, 1], row_wave * inverse_table[:, 0]], axis=1
+    )
+    rows = slab_rows(received, group_size, cross_part, inverse_table, 5)
+    slope = slab_rows(
+        received[..., 2 * depth_keep : 3 * depth_keep], group_size, cross_part, slope_table, 1
+    )
+    kz = lax.broadcasted_iota(jnp.int32, (depth_keep, 1), 0).astype(jnp.float32)
+    strips = jnp.stack(
+        [
+            rows[:, :, 0],
+            rows[:, :, 1],
+            rows[:, :, 2],
+            slope[:, :, 0] - turned(kz * rows[:, :, 1]),
+            turned(kz * rows[:, :, 0]) - rows[:, :, 3],
+            rows[:, :, 4],
+        ],
+        axis=2,
+    )
+    physical = jnp.einsum("sxcjy,sjz->cxyz", strips, backward_cut, precision=highest)
     velocity = physical[:3]
     vorticity = physical[3:]
     nonlinear = jnp.stack(
@@ -167,13 +183,11 @@
     energy = 0.5 * summed / float(points**3)
     layers = slab_planes(nonlinear, group_size, cross_part, onward_cut, forward_table)
     spectra = slab_close(
-        lax.all_to_all(layers, ("py", "pz"), split_axis=2, concat_axis=2, tiled=True),
+        lax.all_to_all(layers, ("py", "pz"), split_axis=0, concat_axis=0, tiled=True),
         group_size,
-        depth_keep,
-        cross_part,
         slab_width,
         forward_table,
-    )
+    ).reshape(2, 3, depth_keep, cross_part, points)
     spectra = jnp.concatenate(
         [spectra, jnp.zeros((2, 3, half_depth - depth_keep, cross_part, points), jnp.float32)],
         axis=2,

time: 1050 us -> 607 us (0.58)
  local copies, waits for them, and re-layouts: 424 us -> 132 us
  matrix products: 279 us -> 96.7 us
  blocking collectives: 46.7 us -> 98 us
    reshape x7 -> x0, local copies, waits for them, and re-layouts: 315 us -> none  [the longest x2 114 us: slab_spread(): spread.reshape(2, components, group_size, depth_part * cross_part * slab_...]
    dot_general x6 -> x7, matrix products: 279 us -> 96.7 us  [the longest x2 26.7 us: slab_rows(): jnp.einsum('grxlm,rsgly->sxmy', received, table.reshape(2, 2, group_size,...]
    transpose x0 -> x5, local copies, waits for them, and re-layouts: none -> 52.2 us  [the longest x1 16.9 us: slab_rows(): jnp.einsum('grxlm,rsgly->sxmy', received, table.reshape(2, 2, group_size,...]
    psum x1, blocking collectives: 32.4 us -> 83.7 us  [on_device(): summed = lax.psum(local_squares, ('py', 'pz'))]
    sub x3 -> x0, other arithmetic: 42.8 us -> none  [the longest x1 22.7 us: on_device(): waves[2] * solenoidal[:, 0] - waves[0] * solenoidal[:, 2]]
    mul x6 -> x0, local copies, waits for them, and re-layouts: 39 us -> none  [project(): keep_mask * (field[:, axis_index] - waves[axis_index] * normal_part * inv...]
    mul x2 -> x4, other arithmetic: 7.29 us -> 29.3 us  [project(): keep_mask * (field[:, axis_index] - waves[axis_index] * normal_part * inv...]
    all_to_all x0 -> x1, local copies, waits for them, and re-layouts: none -> 12.8 us  [on_device(): lax.all_to_all(slab_spread(fields, group_size, slab_width, inverse_table)...]
where the time goes in v1:
time: 607 us; the launch traced here: 596 us
  waiting for transfers between devices  149 us (25%)
  local copies, waits for them, and re-layouts  132 us (22%)
  other arithmetic  102 us (17%)
  blocking collectives  98 us (16%)
  matrix products  96.7 us (16%)
  starting transfers between devices  11.2 us (2%)
  between operations  6.98 us (1%)
    all_to_all x1, waiting for transfers between devices, on_device(): lax.all_to_all(slab_spread(fields, group_size, slab_width, inverse_table)...  149 us
    psum x1, blocking collectives, on_device(): summed = lax.psum(local_squares, ('py', 'pz'))  83.7 us
    another operation x6, local copies, waits for them, and re-layouts, project(): jnp.stack([keep_mask * (field[:, axis_index] - waves[axis_index] * normal...  33.3 us
    mul x4, other arithmetic, project(): keep_mask * (field[:, axis_index] - waves[axis_index] * normal_part * inv...  29.3 us
    dot_general x2, matrix products, slab_rows(): jnp.einsum('grxlm,rsgly->sxmy', received, table.reshape(2, 2, group_size,...  26.7 us
    dot_general x1, matrix products, on_device(): jnp.einsum('sxcjy,sjz->cxyz', strips, backward_cut, precision=highest)  21.9 us
    reduce_max x1, other arithmetic, on_device(): jnp.max(jnp.abs(velocity[0]) + jnp.abs(velocity[1]) + jnp.abs(velocity[2]))  17.2 us
    transpose x1, local copies, waits for them, and re-layouts, slab_rows(): jnp.einsum('grxlm,rsgly->sxmy', received, table.reshape(2, 2, group_size,...  16.9 us
  transfers between devices with their start and end apart: 2, of which 1 were waited for; matrix products, arithmetic and copies ran while one was open for 6% of the time, Pallas kernels for 0%

profile of v1, /device:TPU:0, one launch (start us, length us, event | category | flops | bytes accessed | tf_op | source)
XLA Modules:
  0.0 595.8 jit_solution(1255996920480460246)
XLA Ops:
  5.8 9.4 %copy.67 = f32[2,3,96,4608]{3,2,0,1:T(8,128)} copy(f32[2,3,96,4608]{3,2,1,0:T(8,128)} %param.4) | data formatting | bytes 21233664 | tf_op args[0]
  15.2 13.5 %reshape.541 = f32[2,3,96,24,192]{4,3,2,0,1:T(8,128)} reshape(f32[2,3,96,4608]{3,2,0,1:T(8,128)} %copy.67) | data formatting | bytes 21233664 | tf_op jit(solution)/shard_map/reshape | solution.py:129
  29.8 9.6 %fusion.43 = (f32[2,1,96,24,192]{4,3,2,1,0:T(8,128)S(1)}, f32[2,1,96,24,192]{4,3,2,0,1:T(8,128)}) fusion(f32[2,3,96,24,192]{4,3,2,0,1:T(8,128)} %reshape.541, f32[96,24,192]{2,1,0:T(8,128)S(1)} %maximum_divide_fusion, f32[192]{0:T(256)S(1)} %fusion.130, f32[96,24,192]{2,1,0:T(8,128)S(1)} %and_convert_fusion, f32[96]{0:T(128)S(1)} %iota_convert_fusion.1, ...), kind=kLoop, calls=%fused_computation.57 | loop fusion | flops 7962624 | bytes 21234912 | tf_op jit(solution)/shard_map/mul | solution.py:121
  43.8 6.0 %bitcast_multiply_fusion.3 = (f32[2,1,96,24,192]{4,3,2,0,1:T(8,128)}, f32[2,1,96,24,192]{4,3,2,0,1:T(8,128)S(1)}) fusion(f32[2,1,96,24,192]{4,3,2,0,1:T(8,128)} %get-tuple-element.6, f32[2,3,96,24,192]{4,3,2,0,1:T(8,128)S(1)} %bitcast.254, f32[96,24,192]{2,1,0:T(8,128)} %copy-done.3, f32[24]{0:T(128)S(1)} %fusion.133, f32[96,24,192]{2,1,0:T(8,128)} %copy-done.5, ...), kind=kLoop, calls=%fused_computation.37 | loop fusion | flops 7077888 | bytes 21234144 | tf_op jit(solution)/shard_map/mul | solution.py:121
  49.8 6.2 %fusion.53 = (f32[2,72,24,192]{3,2,1,0:T(8,128)S(1)}, f32[2,72,24,192]{3,2,1,0:T(8,128)}) fusion(f32[2,1,96,24,192]{4,3,2,0,1:T(8,128)S(1)} %get-tuple-element.12, f32[192]{0:T(256)S(1)} %fusion.130, f32[2,1,96,24,192]{4,3,2,1,0:T(8,128)S(1)} %get-tuple-element.5, f32[24]{0:T(128)S(1)} %fusion.133, f32[2,1,96,24,192]{4,3,2,0,1:T(8,128)} %get-tuple-element.11), kind=kLoop, calls=%fused_computation.78 | loop fusion | flops 2654208 | bytes 13271904 | tf_op jit(solution)/shard_map/mul | solution.py:135
  67.9 16.5 %fusion.30 = f32[8,2,24,24,360]{4,2,3,0,1:T(8,128)} fusion(f32[2,360,24,192,1,1]{3,2,1,0,5,4:T(8,128)S(1)} %bitcast.262, f32[1,1,192,8,24]{2,4,0,3,1:T(8,128)S(1)} %get-tuple-element.38, f32[1,1,192,8,24]{2,4,0,3,1:T(8,128)S(1)} %get-tuple-element.36, f32[1,1,192,8,24]{2,4,0,3,1:T(8,128)S(1)} %get-tuple-element.37), kind=kOutput, calls=%fused_computation.41 | convolution fusion | flops 7644561408 | bytes 26984448 | tf_op jit(solution)/shard_map/rmlk,rskgx->gsxlm/dot_general | solution.py:37
  84.3 11.4 %copy.83 = f32[8,2,24,24,360]{4,2,3,1,0:T(8,128)} copy(f32[8,2,24,24,360]{4,2,3,0,1:T(8,128)} %fusion.30) | data formatting | bytes 26542080 | tf_op jit(solution)/shard_map/rmlk,rskgx->gsxlm/transpose | solution.py:37
  108.1 149.1 %all-to-all-done = f32[8,2,24,24,360]{4,2,3,1,0:T(8,128)} async-done(((f32[8,2,24,24,360]{4,2,3,1,0:T(8,128)}), f32[8,2,24,24,360]{4,2,3,1,0:T(8,128)}, u32[]{:S(2)}, u32[]{:S(2)}) %all-to-all-start) | async-done | bytes 13271072 | tf_op jit(solution)/shard_map/all_to_all | solution.py:140
  257.1 19.2 %fusion.27 = f32[2,24,360,192]{2,3,1,0:T(8,128)} fusion(f32[1,1,8,24,192]{4,3,0,2,1:T(8,128)S(1)} %get-tuple-element.33, f32[1,1,8,24,192]{4,3,0,2,1:T(8,128)S(1)} %get-tuple-element.31, f32[1,1,8,24,192]{4,3,0,2,1:T(8,128)S(1)} %get-tuple-element.32, f32[8,2,24,24,360]{4,2,3,1,0:T(8,128)} %all-to-all-done), kind=kOutput, calls=%fused_computation.40 | convolution fusion | flops 7644561408 | bytes 26984448 | tf_op jit(solution)/shard_map/grxlm,rsgly->sxmy/dot_general | solution.py:47
  276.3 16.9 %copy.85 = f32[2,24,360,192]{3,2,1,0:T(8,128)} copy(f32[2,24,360,192]{2,3,1,0:T(8,128)} %fusion.27) | data formatting | bytes 26542080 | tf_op jit(solution)/shard_map/grxlm,rsgly->sxmy/transpose | solution.py:47
  299.3 12.8 %copy.84 = f32[8,2,24,24,360]{4,3,1,0,2:T(8,128)} copy(f32[8,2,24,24,360]{4,2,3,1,0:T(8,128)} %all-to-all-done) | data formatting | bytes 26542080 | tf_op jit(solution)/shard_map/all_to_all | solution.py:140
  312.1 7.6 %fusion.54 = f32[2,24,1,72,192]{4,3,1,0,2:T(8,128)S(1)} fusion(f32[1,24,72,192]{3,2,1,0:T(8,128)S(1)} %get-tuple-element.18, f32[1,24,72,192]{3,2,1,0:T(8,128)S(1)} %get-tuple-element.17, f32[8,2,24,24,360]{4,3,1,0,2:T(8,128)} %copy.84, f32[2,1,8,24,192]{4,3,2,0,1:T(8,128)} %bitcast.271, f32[2,1,8,24,192]{4,3,2,0,1:T(8,128)} %bitcast.270), kind=kOutput, calls=%fused_computation.82 | convolution fusion | flops 1530298368 | bytes 10813440 | tf_op jit(solution)/shard_map/grxlm,rsgly->sxmy/dot_general | solution.py:47
  319.7 21.9 %fusion.17 = f32[6,24,192,192]{2,3,0,1:T(8,128)} fusion(f32[1,96,192]{2,1,0:T(8,128)S(1)} %copy-done.22, f32[1,96,192]{2,1,0:T(8,128)S(1)} %copy-done.23, f32[2,24,1,72,192]{4,3,1,0,2:T(8,128)S(1)} %fusion.54, f32[2,24,5,72,192]{4,3,2,1,0:T(8,128)} %bitcast.261, f32[1,24,1,72,192]{4,3,1,2,0:T(8,128)S(1)} %copy-done.9, f32[1,24,1,72,192]{4,3,1,2,0:T(8,128)S(1)} %copy-done.8), kind=kOutput, calls=%fused_computation.24 | convolution fusion | flops 4599797760 | bytes 39960576 | tf_op jit(solution)/shard_map/sxcjy,sjz->cxyz/dot_general | solution.py:169
  341.5 17.2 %add_reduce_fusion = (f32[]{:T(128)}, f32[1,24,192,192]{2,3,0,1:T(8,128)}, f32[1,24,192,192]{2,3,0,1:T(8,128)}, f32[1,24,192,192]{2,3,0,1:T(8,128)}) fusion(f32[6,24,192,192]{2,3,0,1:T(8,128)} %fusion.17), kind=kLoop, calls=%fused_computation.59 | loop fusion | flops 13271039 | bytes 31850500 | tf_op jit(solution)/shard_map/reduce_max | solution.py:179
  358.7 8.2 %fusion.44 = f32[2,24,3,72,192]{4,3,1,2,0:T(8,128)S(1)} fusion(f32[192,1,96]{0,2,1:T(8,128)S(1)} %copy-done.10, f32[192,1,96]{0,2,1:T(8,128)S(1)} %copy-done.11, f32[1,24,192,192]{2,3,0,1:T(8,128)} %get-tuple-element.10, f32[1,24,192,192]{2,3,0,1:T(8,128)} %get-tuple-element.8, f32[1,24,192,192]{2,3,0,1:T(8,128)} %get-tuple-element.9), kind=kOutput, calls=%fused_computation.65 | convolution fusion | flops 2298599424 | bytes 18726912 | tf_op jit(solution)/shard_map/cxyz,zrj->rxcjy/dot_general | solution.py:59
  371.8 10.6 %convolution_bitcast_fusion = f32[8,2,24,24,216]{4,3,2,0,1:T(8,128)S(1)} fusion(f32[2,24,216,192,1,1]{3,2,1,0,5,4:T(8,128)} %bitcast.269, f32[1,1,192,8,24]{2,4,0,3,1:T(8,128)S(1)} %copy-done.17, f32[1,1,192,8,24]{2,4,0,3,1:T(8,128)S(1)} %copy-done.15, f32[1,1,192,8,24]{2,4,0,3,1:T(8,128)S(1)} %copy-done.14), kind=kOutput, calls=%fused_computation.84 | convolution fusion | flops 4586913792 | bytes 16367616 | tf_op jit(solution)/shard_map/rxmy,rsygl->gsxlm/dot_general | solution.py:60
  382.5 6.6 %copy.100 = f32[8,2,24,24,216]{4,2,1,3,0:T(8,128)} copy(f32[8,2,24,24,216]{4,3,2,0,1:T(8,128)S(1)} %convolution_bitcast_fusion) | data formatting | bytes 15925248 | tf_op jit(solution)/shard_map/rxmy,rsygl->gsxlm/transpose | solution.py:60
  413.3 9.3 %fusion.12 = f32[]{:T(128)} fusion(f32[6,24,192,192]{2,3,0,1:T(8,128)} %fusion.17), kind=kLoop, calls=%fused_computation.18 | loop fusion | flops 5308415 | bytes 10616836 | tf_op jit(solution)/shard_map/reduce_sum | solution.py:180
  423.3 83.7 %psum.7 = f32[]{:T(128)} all-reduce(f32[]{:T(128)} %fusion.12), channel_id=1, replica_groups=mesh['member'=4,'py'=4,'pz'=2] {'py','pz'}, use_global_device_ids=true, to_apply=%region_1.2 | all-reduce | flops 1 | bytes 8 | tf_op jit(solution)/shard_map/psum | solution.py:182
  506.9 14.3 %pmax.7 = f32[]{:T(128)} all-reduce(f32[]{:T(128)} %get-tuple-element.7), channel_id=1, replica_groups=mesh['member'=4,'py'=4,'pz'=2] {'py','pz'}, use_global_device_ids=true, to_apply=%region_3.4 | all-reduce | flops 1 | bytes 8 | tf_op jit(solution)/shard_map/pmax | solution.py:181
  523.2 12.9 %fusion.55 = f32[2,216,24,192]{1,3,2,0:T(8,128)} fusion(f32[8,2,24,24,216]{4,2,1,3,0:T(8,128)} %all-to-all-done.1, f32[1,1,8,24,192]{4,3,0,2,1:T(8,128)S(1)} %copy-done.21, f32[1,1,8,24,192]{4,3,0,2,1:T(8,128)S(1)} %copy-done.19, f32[1,1,8,24,192]{4,3,0,2,1:T(8,128)S(1)} %copy-done.18), kind=kOutput, calls=%fused_computation.83 | convolution fusion | flops 4586913792 | bytes 16367616 | tf_op jit(solution)/shard_map/gsxlm,srgxk->rmlk/dot_general | solution.py:70
  536.0 12.4 %copy.102 = f32[2,216,24,192]{3,2,1,0:T(8,128)} copy(f32[2,216,24,192]{1,3,2,0:T(8,128)} %fusion.55) | data formatting | bytes 15925248 | tf_op jit(solution)/shard_map/gsxlm,srgxk->rmlk/transpose | solution.py:70
  548.5 9.1 %subtract_multiply_fusion.1 = (f32[2,1,96,24,192]{4,3,2,1,0:T(8,128)}, f32[2,1,96,24,192]{4,3,2,1,0:T(8,128)S(1)}) fusion(f32[2,3,72,24,192]{4,3,2,1,0:T(8,128)} %bitcast.255, f32[96,24,192]{2,1,0:T(8,128)S(1)} %copy-done.4, f32[192]{0:T(256)S(1)} %copy-done.25, f32[96,24,192]{2,1,0:T(8,128)} %copy-done.5, f32[96]{0:T(128)S(1)} %copy-done.29, ...), kind=kLoop, calls=%fused_computation.61 | loop fusion | flops 7962624 | bytes 18580704 | tf_op jit(solution)/shard_map/mul | solution.py:121
  581.2 12.0 %fusion.23 = f32[2,3,96,4608]{3,2,1,0:T(8,128)} fusion(f32[2,1,96,4608]{3,2,1,0:T(8,128)} %bitcast.268, f32[2,1,96,4608]{3,2,1,0:T(8,128)} %bitcast.267, f32[2,1,96,4608]{3,2,1,0:T(8,128)} %bitcast.266, f32[2,1,96,4608]{3,2,1,0:T(8,128)} %bitcast.264, f32[2,1,96,4608]{3,2,1,0:T(8,128)S(1)} %bitcast.263, f32[2,1,96,4608]{3,2,1,0:T(8,128)} %bitcast.265, ...), kind=kLoop, calls=%fused_computation.30 | loop fusion | flops 31850496 | bytes 33619976 | tf_op jit(solution)/shard_map/add | solution.py:201
  (126 shorter events, 92.5 us)
Async XLA Ops:
  0.6 38.8 %copy-start.28 = (f32[96]{0:T(128)}, f32[96]{0:T(128)S(1)}, u32[]{:S(2)}) copy-start(f32[96]{0:T(128)S(1)} %iota_convert_fusion.1) | copy-start | bytes 1156
  0.7 28.2 %copy-start.30 = (f32[96]{0:T(128)}, f32[96]{0:T(128)S(1)}, u32[]{:S(2)}) copy-start(f32[96]{0:T(128)S(1)} %fusion.134) | copy-start | bytes 1156
  0.7 49.1 %copy-start.26 = (f32[24]{0:T(128)}, f32[24]{0:T(128)S(1)}, u32[]{:S(2)}) copy-start(f32[24]{0:T(128)S(1)} %fusion.133) | copy-start | bytes 292
  0.7 104.7 %copy-start.24 = (f32[192]{0:T(256)}, f32[192]{0:T(256)S(1)}, u32[]{:S(2)}) copy-start(f32[192]{0:T(256)S(1)} %fusion.130) | copy-start | bytes 2308
  5.8 62.1 %copy-start.16 = (f32[1,1,192,8,24]{2,4,0,3,1:T(8,128)}, f32[1,1,192,8,24]{2,4,0,3,1:T(8,128)S(1)}, u32[]{:S(2)}) copy-start(f32[1,1,192,8,24]{2,4,0,3,1:T(8,128)S(1)} %get-tuple-element.38) | copy-start | bytes 442372
  29.7 10.8 %slice-start.1 = ((s8[14155776]{0:T(1024)(128)(4,1)}), s8[4194304]{0:T(1024)(128)(4,1)S(1)}, s32[]{:S(2)}) async-start(s8[14155776]{0:T(1024)(128)(4,1)} %bitcast.253), calls=%async_computation.3 | async-start | bytes 8388608
  29.7 13.6 %slice-start.2 = ((s8[14155776]{0:T(1024)(128)(4,1)}), s8[4194304]{0:T(1024)(128)(4,1)S(1)}, s32[]{:S(2)}) async-start(s8[14155776]{0:T(1024)(128)(4,1)} %bitcast.253), calls=%async_computation.4 | async-start | bytes 8388608
  29.7 14.0 %slice-start.3 = ((s8[14155776]{0:T(1024)(128)(4,1)}), s8[1572864]{0:T(1024)(128)(4,1)S(1)}, s32[]{:S(2)}) async-start(s8[14155776]{0:T(1024)(128)(4,1)} %bitcast.253), calls=%async_computation.5 | async-start | bytes 3145728
  39.4 21.6 %copy-start.1 = (f32[2,1,96,24,192]{4,3,2,1,0:T(8,128)}, f32[2,1,96,24,192]{4,3,2,1,0:T(8,128)S(1)}, u32[]{:S(2)}) copy-start(f32[2,1,96,24,192]{4,3,2,1,0:T(8,128)S(1)} %get-tuple-element.5) | copy-start | bytes 10616836
  49.8 11.2 %copy-start.2 = (f32[2,1,96,24,192]{4,3,2,0,1:T(8,128)}, f32[2,1,96,24,192]{4,3,2,0,1:T(8,128)S(1)}, u32[]{:S(2)}) copy-start(f32[2,1,96,24,192]{4,3,2,0,1:T(8,128)S(1)} %get-tuple-element.12) | copy-start | bytes 10616836
  95.7 161.4 %all-to-all-start = ((f32[8,2,24,24,360]{4,2,3,1,0:T(8,128)}), f32[8,2,24,24,360]{4,2,3,1,0:T(8,128)}, u32[]{:S(2)}, u32[]{:S(2)}) async-start(f32[8,2,24,24,360]{4,2,3,1,0:T(8,128)} %copy.83), calls=%async_computation | async-start | bytes 28311552 | tf_op jit(solution)/shard_map/all_to_all | solution.py:140
  108.1 168.3 %copy-start.20 = (f32[1,1,8,24,192]{4,3,0,2,1:T(8,128)}, f32[1,1,8,24,192]{4,3,0,2,1:T(8,128)S(1)}, u32[]{:S(2)}) copy-start(f32[1,1,8,24,192]{4,3,0,2,1:T(8,128)S(1)} %get-tuple-element.33) | copy-start | bytes 442372
  341.5 17.2 %copy-start.10 = (f32[192,1,96]{0,2,1:T(8,128)S(1)}, f32[192,1,96]{0,2,1:T(8,128)}, u32[]{:S(2)}) copy-start(f32[192,1,96]{0,2,1:T(8,128)} %get-tuple-element.50) | copy-start | bytes 221188
  341.5 17.2 %copy-start.11 = (f32[192,1,96]{0,2,1:T(8,128)S(1)}, f32[192,1,96]{0,2,1:T(8,128)}, u32[]{:S(2)}) copy-start(f32[192,1,96]{0,2,1:T(8,128)} %get-tuple-element.51) | copy-start | bytes 221188
  389.0 134.1 %all-to-all-start.1 = ((f32[8,2,24,24,216]{4,2,1,3,0:T(8,128)}), f32[8,2,24,24,216]{4,2,1,3,0:T(8,128)}, u32[]{:S(2)}, u32[]{:S(2)}) async-start(f32[8,2,24,24,216]{4,2,1,3,0:T(8,128)} %copy.100), calls=%async_computation.1 | async-start | bytes 18874368 | tf_op jit(solution)/shard_map/all_to_all | solution.py:186
  413.3 109.9 %copy-start.18 = (f32[1,1,8,24,192]{4,3,0,2,1:T(8,128)S(1)}, f32[1,1,8,24,192]{4,3,0,2,1:T(8,128)}, u32[]{:S(2)}) copy-start(f32[1,1,8,24,192]{4,3,0,2,1:T(8,128)} %get-tuple-element.29) | copy-start | bytes 442372
  413.3 109.9 %copy-start.19 = (f32[1,1,8,24,192]{4,3,0,2,1:T(8,128)S(1)}, f32[1,1,8,24,192]{4,3,0,2,1:T(8,128)}, u32[]{:S(2)}) copy-start(f32[1,1,8,24,192]{4,3,0,2,1:T(8,128)} %get-tuple-element.30) | copy-start | bytes 442372
  413.3 109.9 %copy-start.21 = (f32[1,1,8,24,192]{4,3,0,2,1:T(8,128)S(1)}, f32[1,1,8,24,192]{4,3,0,2,1:T(8,128)}, u32[]{:S(2)}) copy-start(f32[1,1,8,24,192]{4,3,0,2,1:T(8,128)} %copy-done.20) | copy-start | bytes 442372
  536.0 12.4 %copy-start.4 = (f32[96,24,192]{2,1,0:T(8,128)S(1)}, f32[96,24,192]{2,1,0:T(8,128)}, u32[]{:S(2)}) copy-start(f32[96,24,192]{2,1,0:T(8,128)} %copy-done.3) | copy-start | bytes 5308420
  536.0 12.4 %copy-start.25 = (f32[192]{0:T(256)S(1)}, f32[192]{0:T(256)}, u32[]{:S(2)}) copy-start(f32[192]{0:T(256)} %copy-done.24) | copy-start | bytes 2308
  536.0 12.4 %copy-start.27 = (f32[24]{0:T(128)S(1)}, f32[24]{0:T(128)}, u32[]{:S(2)}) copy-start(f32[24]{0:T(128)} %copy-done.26) | copy-start | bytes 292
  536.0 12.4 %copy-start.29 = (f32[96]{0:T(128)S(1)}, f32[96]{0:T(128)}, u32[]{:S(2)}) copy-start(f32[96]{0:T(128)} %copy-done.28) | copy-start | bytes 1156
  548.5 10.6 %copy-start = (f32[2,216,24,192]{3,2,1,0:T(8,128)S(1)}, f32[2,216,24,192]{3,2,1,0:T(8,128)}, u32[]{:S(2)}) copy-start(f32[2,216,24,192]{3,2,1,0:T(8,128)} %copy.102) | copy-start | bytes 23887876
  548.5 11.3 %copy-start.6 = (f32[96,24,192]{2,1,0:T(8,128)S(1)}, f32[96,24,192]{2,1,0:T(8,128)}, u32[]{:S(2)}) copy-start(f32[96,24,192]{2,1,0:T(8,128)} %copy-done.5) | copy-start | bytes 5308420
  (16 other events, 99.8 us)
